TPU v7x, 32 devices: a whole 2x2x4 slice. The times are simulated.
32 devices in a mesh: groups: 2 (over y), ga: 16 (over z, x, core).
Axes of the slice: x: 2, y: 2, z: 4, core: 2. Of those that a mesh axis runs over, the one named last changes fastest.
Arguments:
- occupied: float32 [2, 1024, 12288], P(None, None, 'ga'), may hold values from -0.0546875 to 0.0546875
- residual: float32 [4, 2, 128, 12288], P('groups', None, None, 'ga'), parts along dimension 0, may hold values from -6 to 6
- old_direction: float32 [4, 2, 128, 12288], P('groups', None, None, 'ga'), parts along dimension 0, may hold values from -6 to 6
- kin_ratio: float32 [12288], P('ga'), may hold values from 0.06 to 5, as said below
- old_dot: float32 [4, 128], P('groups'), parts along dimension 0, may hold values from 6144 to 24576
Outputs:
- direction: float32 [4, 2, 128, 12288], P('groups', None, None, 'ga'), parts along dimension 0
- dot_new: float32 [4, 128], P('groups'), parts along dimension 0
There are 2 independent parts, one for each index of `groups`. A program takes and returns all parts, laid end to end along the dimension named above; an argument that names none is the same for every part. Nothing has to cross between parts.
Inputs may be any that keep to these rules, and one draw needn't show every extreme that they name: `kin_ratio`: positive; grows with the plane-wave index on average and varies from one plane wave to the next.
All inputs are finite; a program needn't handle non-finite values.
Results may differ from a plain program's by a relative error of at most 0.000056.
Values sent between devices are 32-bit elements; how exact they have to be, the bound alone decides.
No kernel may reach another device: no remote copies, remote signals or barrier semaphores. Data moves between devices by JAX's collectives and lax.ppermute only.
A program may use at most 64 MiB of HBM per device.

v0:
```python
import jax
import jax.numpy as jnp
from jax import lax
from jax.sharding import PartitionSpec as P

highest = lax.Precision.HIGHEST


def teter_factor(ratio):
    numerator = 27.0 + 18.0 * ratio + 12.0 * ratio**2 + 8.0 * ratio**3
    return numerator / (numerator + 16.0 * ratio**4)


def margins(occupied, vectors):
    products = jnp.einsum("hng,pcbg->phcnb", occupied, vectors, precision=highest)
    real_part = products[:, 0, 0] + products[:, 1, 1]
    imag_part = products[:, 0, 1] - products[:, 1, 0]
    return jnp.stack([real_part, imag_part], axis=1)


def correction(summed, occ_rows):
    real_part = summed[:, 0]
    imag_part = summed[:, 1]
    coefficient = jnp.stack(
        [jnp.stack([real_part, -imag_part], axis=1), jnp.stack([imag_part, real_part], axis=1)],
        axis=1,
    )
    return jnp.einsum("pchnb,hng->pcbg", coefficient, occ_rows, precision=highest)


def on_device(occupied, residual, old_direction, kin_ratio, old_dot):
    factor = teter_factor(kin_ratio)
    first = margins(occupied, residual)
    first_total = lax.psum(first, "ga")
    gradient = residual - correction(first_total, occupied)
    precond = factor * gradient
    local_dot = jnp.sum(factor * (gradient[:, 0] ** 2 + gradient[:, 1] ** 2), axis=-1)
    second = margins(occupied, precond)
    second_total, dot_new = lax.psum((second, local_dot), "ga")
    projected = precond - correction(second_total, occupied)
    direction = projected + (dot_new / old_dot)[:, None, :, None] * old_direction
    return (direction, dot_new)


def solution(mesh):
    placed = (
        P(None, None, "ga"),
        P("groups", None, None, "ga"),
        P("groups", None, None, "ga"),
        P("ga"),
        P("groups", None),
    )
    return jax.shard_map(
        on_device,
        mesh=mesh,
        in_specs=placed,
        out_specs=(P("groups", None, None, "ga"), P("groups", None)),
        check_vma=False,
    )
```

profile of v0, /device:TPU:0, one launch (start us, length us, event | category | flops | bytes accessed | tf_op | source)
XLA Modules:
  0.0 279.0 jit_solution(1500607859630223277)
XLA Ops:
  7.2 0.0 all-reduce.3.cloned.1.call-start
  7.2 13.1 %fusion.10 = f32[2,2,2,1024,128]{3,4,1,2,0:T(8,128)S(1)} fusion(f32[2,1024,768]{2,1,0:T(8,128)} %param.5, f32[2,2,128,768]{3,2,1,0:T(8,128)} %param.6), kind=kOutput, calls=%fused_computation.12 | convolution fusion | flops 9663676416 | bytes 12058624 | tf_op jit(solution)/shard_map/hng,pcbg->phcnb/dot_general | solution.py:15
  20.4 0.2 fusion.31
  20.5 0.2 fusion.33
  20.7 1.4 pad_maximum_fusion.2
  22.1 0.0 all-reduce.3.cloned.1.call-update
  22.2 0.2 all-reduce.5.cloned.1.call-start
  22.4 0.4 copy-done.3
  22.8 100.4 %all-reduce.3.cloned.1.call-done = f32[2,2,1024,128]{2,3,0,1:T(8,128)} async-done(((f32[2,2,1024,128]{2,3,0,1:T(8,128)}), f32[2,2,1024,128]{2,3,0,1:T(8,128)}) %all-reduce.3.cloned.1.call-update) | async-done | bytes 2097168 | tf_op jit(solution)/shard_map/psum | solution.py:34
  123.2 1.9 slice_negate_fusion.1
  125.1 0.0 copy-start
  125.1 0.0 slice-start
  125.2 0.5 maximum_bitcast_fusion
  125.7 0.9 copy-done
  126.6 16.2 %bitcast_subtract_fusion.1 = f32[2,2,128,768]{3,2,1,0:T(8,128)S(1)} fusion(f32[2,2,128,768]{3,2,1,0:T(8,128)S(1)} %copy-done, f32[2,1024,768]{2,1,0:T(8,128)} %param.5, f32[2,1,2,1024,128]{3,4,0,2,1:T(8,128)S(1)} %get-tuple-element.11, f32[2,1,2,1024,128]{3,4,0,2,1:T(8,128)S(1)} %get-tuple-element.10), kind=kOutput, calls=%fused_computation.24 | convolution fusion | flops 9665118208 | bytes 13631488 | tf_op jit(solution)/shard_map/pchnb,hng->pcbg/dot_general | solution.py:28
  142.7 0.0 slice-done
  142.8 0.0 slice-done.1
  142.8 10.2 %fusion.13 = f32[2,2,2,1024,128]{3,4,1,2,0:T(8,128)S(1)} fusion(f32[2,1024,768]{2,1,0:T(8,128)S(1)} %bitcast.84, f32[2,2,128,768]{3,2,1,0:T(8,128)S(1)} %bitcast_subtract_fusion.1, f32[768]{0:T(1024)S(1)} %add_divide_fusion), kind=kOutput, calls=%fused_computation.13 | convolution fusion | flops 9664069632 | bytes 12061696 | tf_op jit(solution)/shard_map/hng,pcbg->phcnb/dot_general | solution.py:15
  153.0 0.2 fusion.28
  153.1 0.2 fusion.30
  153.3 1.4 pad_maximum_fusion.3
  154.7 0.0 all-reduce.5.cloned.1.call-update
  154.8 0.2 fusion.37
  155.0 31.1 %psum.23 = f32[2,128]{1,0:T(2,128)S(1)} all-reduce(f32[2,128]{1,0:T(2,128)S(1)} %fusion.37), channel_id=1, replica_groups=mesh['groups'=2,'ga'=16] {'ga'}, use_global_device_ids=true, to_apply=%region_3.0 | all-reduce | flops 256 | bytes 2048 | tf_op jit(solution)/shard_map/psum | solution.py:39
  186.1 0.0 copy-done.4
  186.1 66.3 %all-reduce.5.cloned.1.call-done = f32[2,2,1024,128]{2,3,0,1:T(8,128)} async-done(((f32[2,2,1024,128]{2,3,0,1:T(8,128)}), f32[2,2,1024,128]{2,3,0,1:T(8,128)}) %all-reduce.5.cloned.1.call-update) | async-done | bytes 2097168 | tf_op jit(solution)/shard_map/psum | solution.py:39
  252.5 1.9 slice_negate_fusion
  254.4 0.0 copy-done.2
  254.4 0.0 copy-start.1
  254.4 0.5 maximum_bitcast_fusion.2
  254.9 0.9 copy-done.1
  255.8 16.4 %fusion.18 = f32[2,2,128,768]{3,2,1,0:T(8,128)} fusion(f32[2,2,128,768]{3,2,1,0:T(8,128)S(1)} %copy-done.1, f32[2,1024,768]{2,1,0:T(8,128)} %param.5, f32[2,2,128,768]{3,2,1,0:T(8,128)S(1)} %bitcast_subtract_fusion.1, f32[2,128]{1,0:T(2,128)S(1)} %div.7, f32[768]{0:T(1024)S(1)} %add_divide_fusion, f32[2,1,2,1024,128]{3,4,0,2,1:T(8,128)S(1)} %get-tuple-element.9, ...), kind=kOutput, calls=%fused_computation.23 | convolution fusion | flops 9666297856 | bytes 15208448 | tf_op jit(solution)/shard_map/pchnb,hng->pcbg/dot_general | solution.py:28
  (7 shorter events, 0.0 us)
Async XLA Ops:
  7.2 116.1 %all-reduce.3.cloned.1.call-start = ((), (), s32[]{:S(2)}) async-start(), calls=%async_computation | async-start | bytes 4194304 | tf_op jit(solution)/shard_map/psum | solution.py:34
  22.1 0.7 copy-start.3
  22.2 230.3 %all-reduce.5.cloned.1.call-start = ((), (), s32[]{:S(2)}) async-start(), calls=%async_computation.1 | async-start | bytes 4194304 | tf_op jit(solution)/shard_map/psum | solution.py:39
  125.1 1.4 copy-start
  125.1 17.6 %slice-start = ((s8[6291456]{0:T(1024)(128)(4,1)}), s8[4194304]{0:T(1024)(128)(4,1)S(1)}, s32[]{:S(2)}) async-start(s8[6291456]{0:T(1024)(128)(4,1)} %bitcast.83), calls=%async_computation.2 | async-start | bytes 8388608
  126.5 16.2 %slice-start.1 = ((s8[6291456]{0:T(1024)(128)(4,1)}), s8[2097152]{0:T(1024)(128)(4,1)S(1)}, s32[]{:S(2)}) async-start(s8[6291456]{0:T(1024)(128)(4,1)} %bitcast.83), calls=%async_computation.3 | async-start | bytes 4194304
  154.7 31.4 %copy-start.4 = (f32[2,128]{1,0:T(2,128)S(1)}, f32[2,128]{1,0:T(2,128)}, u32[]{:S(2)}) copy-start(f32[2,128]{1,0:T(2,128)} %param.9) | copy-start | bytes 3076
  186.1 68.3 %copy-start.2 = (f32[2,128]{1,0:T(2,128)}, f32[2,128]{1,0:T(2,128)S(1)}, u32[]{:S(2)}) copy-start(f32[2,128]{1,0:T(2,128)S(1)} %psum.23) | copy-start | bytes 3076
  254.4 1.4 copy-start.1
Sparse Core Ops, SparseCore 0:
  22.3 100.8 all-reduce.2
  154.9 97.5 all-reduce.4
where the time goes:
time: 279 us
  waiting for transfers between devices  167 us (60%)
  matrix products  55.9 us (20%)
  blocking collectives  31.1 us (11%)
  between operations  14.2 us (5%)
  other arithmetic  8.56 us (3%)
    psum x1, waiting for transfers between devices, on_device(): first_total = lax.psum(first, 'ga')  100 us
    psum x1, waiting for transfers between devices, on_device(): second_total, dot_new = lax.psum((second, local_dot), 'ga')  66.3 us
    dot_general x2, matrix products, correction(): jnp.einsum('pchnb,hng->pcbg', coefficient, occ_rows, precision=highest)  32.6 us
    psum x1, blocking collectives, on_device(): second_total, dot_new = lax.psum((second, local_dot), 'ga')  31.1 us
    dot_general x2, matrix products, margins(): jnp.einsum('hng,pcbg->phcnb', occupied, vectors, precision=highest)  23.3 us
  transfers between devices with their start and end apart: 2, of which 2 were waited for; matrix products, arithmetic and copies ran while one was open for 0% of the time, Pallas kernels for 0%

commit v1 on v0

--- a/solution.py
+++ b/solution.py
@@ -31,7 +31,7 @@
 def on_device(occupied, residual, old_direction, kin_ratio, old_dot):
     factor = teter_factor(kin_ratio)
     first = margins(occupied, residual)
-    first_total = lax.psum(first, "ga")
+    first_total = jnp.sum(lax.all_gather(first, "ga"), axis=0)
     gradient = residual - correction(first_total, occupied)
     precond = factor * gradient
     local_dot = jnp.sum(factor * (gradient[:, 0] ** 2 + gradient[:, 1] ** 2), axis=-1)

time: 279 us -> 360 us (1.29)
  waiting for transfers between devices: 167 us -> 235 us
  other arithmetic: 8.56 us -> 18.9 us
    all_gather x0 -> x1, waiting for transfers between devices: none -> 170 us  [on_device(): first_total = jnp.sum(lax.all_gather(first, 'ga'), axis=0)]
    psum x1 -> x0, waiting for transfers between devices: 100 us -> none  [on_device(): first_total = lax.psum(first, 'ga')]
    reduce_sum x0 -> x1, other arithmetic: none -> 12.1 us  [on_device(): first_total = jnp.sum(lax.all_gather(first, 'ga'), axis=0)]
where the time goes in v1:
time: 360 us
  waiting for transfers between devices  235 us (65%)
  matrix products  55.9 us (16%)
  blocking collectives  33.1 us (9%)
  other arithmetic  18.9 us (5%)
  between operations  14.2 us (4%)
    all_gather x1, waiting for transfers between devices, on_device(): first_total = jnp.sum(lax.all_gather(first, 'ga'), axis=0)  170 us
    psum x1, waiting for transfers between devices, on_device(): second_total, dot_new = lax.psum((second, local_dot), 'ga')  65 us
    psum x1, blocking collectives, on_device(): second_total, dot_new = lax.psum((second, local_dot), 'ga')  33.1 us
    dot_general x2, matrix products, correction(): jnp.einsum('pchnb,hng->pcbg', coefficient, occ_rows, precision=highest)  32.6 us
    dot_general x2, matrix products, margins(): jnp.einsum('hng,pcbg->phcnb', occupied, vectors, precision=highest)  23.3 us
    reduce_sum x1, other arithmetic, on_device(): first_total = jnp.sum(lax.all_gather(first, 'ga'), axis=0)  12.1 us
  transfers between devices with their start and end apart: 2, of which 2 were waited for; matrix products, arithmetic and copies ran while one was open for 0% of the time, Pallas kernels for 0%

profile of v1, /device:TPU:0, one launch (start us, length us, event | category | flops | bytes accessed | tf_op | source)
XLA Modules:
  0.0 360.1 jit_solution(5662769204827494497)
XLA Ops:
  7.2 0.0 all-gather.3.cloned.1.call-start
  7.2 13.1 %fusion.12 = f32[2,2,2,1024,128]{3,4,1,2,0:T(8,128)S(1)} fusion(f32[2,1024,768]{2,1,0:T(8,128)} %param.5, f32[2,2,128,768]{3,2,1,0:T(8,128)} %param.6), kind=kOutput, calls=%fused_computation.13 | convolution fusion | flops 9663676416 | bytes 12058624 | tf_op jit(solution)/shard_map/hng,pcbg->phcnb/dot_general | solution.py:15
  20.4 0.2 fusion.33
  20.5 0.2 fusion.35
  20.7 1.5 pad_maximum_fusion.1
  22.2 0.0 all-gather.3.cloned.1.call-update
  22.2 0.2 all-reduce.2.cloned.1.call-start
  22.4 0.4 copy-done.3
  22.9 170.3 %all-gather.3.cloned.1.call-done = f32[32,2,1024,128]{2,3,0,1:T(8,128)} async-done(((f32[2,2,1024,128]{2,3,0,1:T(8,128)}), f32[32,2,1024,128]{2,3,0,1:T(8,128)}) %all-gather.3.cloned.1.call-update) | async-done | bytes 33554448 | tf_op jit(solution)/shard_map/all_gather | solution.py:34
  193.1 12.1 %reduce_sum.18 = f32[2,2,1024,128]{2,3,0,1:T(8,128)S(1)} reduce(f32[16,2,2,1024,128]{3,4,1,0,2:T(8,128)} %bitcast.94, f32[]{:T(128)} %constant.5.clone.1), dimensions={0}, to_apply=%region_0.0 | reduce | flops 7864320 | bytes 35651588 | tf_op jit(solution)/shard_map/reduce_sum | solution.py:34
  205.2 0.2 slice_bitcast_fusion.2
  205.5 0.1 fusion.46
  205.6 0.0 copy-start
  205.6 0.0 slice-start
  205.6 0.6 maximum_bitcast_fusion
  206.2 0.8 copy-done
  207.0 16.2 %bitcast_subtract_fusion.1 = f32[2,2,128,768]{3,2,1,0:T(8,128)S(1)} fusion(f32[2,2,128,768]{3,2,1,0:T(8,128)S(1)} %copy-done, f32[2,1024,768]{2,1,0:T(8,128)} %param.5, f32[2,1,2,1024,128]{3,4,2,1,0:T(8,128)S(1)} %get-tuple-element.10, f32[2,1,2,1024,128]{3,4,2,1,0:T(8,128)S(1)} %get-tuple-element.9), kind=kOutput, calls=%fused_computation.25 | convolution fusion | flops 9665118208 | bytes 13631488 | tf_op jit(solution)/shard_map/pchnb,hng->pcbg/dot_general | solution.py:28
  223.2 0.0 slice-done
  223.2 0.0 slice-done.1
  223.2 10.2 %fusion.15 = f32[2,2,2,1024,128]{3,4,1,2,0:T(8,128)S(1)} fusion(f32[2,1024,768]{2,1,0:T(8,128)S(1)} %bitcast.93, f32[2,2,128,768]{3,2,1,0:T(8,128)S(1)} %bitcast_subtract_fusion.1, f32[768]{0:T(1024)S(1)} %add_divide_fusion), kind=kOutput, calls=%fused_computation.14 | convolution fusion | flops 9664069632 | bytes 12061696 | tf_op jit(solution)/shard_map/hng,pcbg->phcnb/dot_general | solution.py:15
  233.4 0.2 fusion.30
  233.6 0.2 fusion.32
  233.7 1.4 pad_maximum_fusion.2
  235.2 0.0 all-reduce.2.cloned.1.call-update
  235.2 0.2 fusion.39
  235.4 33.1 %psum.15 = f32[2,128]{1,0:T(2,128)S(1)} all-reduce(f32[2,128]{1,0:T(2,128)S(1)} %fusion.39), channel_id=1, replica_groups=mesh['groups'=2,'ga'=16] {'ga'}, use_global_device_ids=true, to_apply=%region_3.0 | all-reduce | flops 256 | bytes 2048 | tf_op jit(solution)/shard_map/psum | solution.py:39
  268.5 65.0 %all-reduce.2.cloned.1.call-done = f32[2,2,1024,128]{2,3,0,1:T(8,128)} async-done(((f32[2,2,1024,128]{2,3,0,1:T(8,128)}), f32[2,2,1024,128]{2,3,0,1:T(8,128)}) %all-reduce.2.cloned.1.call-update) | async-done | bytes 2097168 | tf_op jit(solution)/shard_map/psum | solution.py:39
  333.5 1.9 slice_negate_fusion
  335.4 0.0 copy-start.1
  335.4 0.5 maximum_bitcast_fusion.2
  335.9 0.9 copy-done.1
  336.8 16.4 %fusion.20 = f32[2,2,128,768]{3,2,1,0:T(8,128)} fusion(f32[2,2,128,768]{3,2,1,0:T(8,128)S(1)} %copy-done.1, f32[2,1024,768]{2,1,0:T(8,128)} %param.5, f32[2,2,128,768]{3,2,1,0:T(8,128)S(1)} %bitcast_subtract_fusion.1, f32[2,128]{1,0:T(2,128)S(1)} %div.7, f32[768]{0:T(1024)S(1)} %add_divide_fusion, f32[2,1,2,1024,128]{3,4,0,2,1:T(8,128)S(1)} %get-tuple-element.8, ...), kind=kOutput, calls=%fused_computation.24 | convolution fusion | flops 9666297856 | bytes 15208448 | tf_op jit(solution)/shard_map/pchnb,hng->pcbg/dot_general | solution.py:28
  (9 shorter events, 0.0 us)
Async XLA Ops:
  7.2 186.0 %all-gather.3.cloned.1.call-start = ((), (), s32[]{:S(2)}) async-start(), calls=%async_computation.1 | async-start | bytes 35651584 | tf_op jit(solution)/shard_map/all_gather | solution.py:34
  22.2 0.7 copy-start.3
  22.2 311.3 %all-reduce.2.cloned.1.call-start = ((), (), s32[]{:S(2)}) async-start(), calls=%async_computation | async-start | bytes 4194304 | tf_op jit(solution)/shard_map/psum | solution.py:39
  205.6 1.4 copy-start
  205.6 17.6 %slice-start = ((s8[6291456]{0:T(1024)(128)(4,1)}), s8[4194304]{0:T(1024)(128)(4,1)S(1)}, s32[]{:S(2)}) async-start(s8[6291456]{0:T(1024)(128)(4,1)} %bitcast.92), calls=%async_computation.2 | async-start | bytes 8388608
  207.0 16.2 %slice-start.1 = ((s8[6291456]{0:T(1024)(128)(4,1)}), s8[2097152]{0:T(1024)(128)(4,1)S(1)}, s32[]{:S(2)}) async-start(s8[6291456]{0:T(1024)(128)(4,1)} %bitcast.92), calls=%async_computation.3 | async-start | bytes 4194304
  235.2 33.3 %copy-start.4 = (f32[2,128]{1,0:T(2,128)S(1)}, f32[2,128]{1,0:T(2,128)}, u32[]{:S(2)}) copy-start(f32[2,128]{1,0:T(2,128)} %param.9) | copy-start | bytes 3076
  268.5 66.9 %copy-start.2 = (f32[2,128]{1,0:T(2,128)}, f32[2,128]{1,0:T(2,128)S(1)}, u32[]{:S(2)}) copy-start(f32[2,128]{1,0:T(2,128)S(1)} %psum.15) | copy-start | bytes 3076
  335.4 1.4 copy-start.1
Sparse Core Ops, SparseCore 0:
  22.3 170.7 all-gather.2
  235.3 98.1 all-reduce.1
